TPU v7x, 32 devices: a whole 2x2x4 slice. The times are simulated.
32 devices in a mesh: ep: 8 (over z, x), tp: 4 (over y, core).
Axes of the slice: x: 2, y: 2, z: 4, core: 2. Of those that a mesh axis runs over, the one named last changes fastest.
Arguments:
- tokens: bfloat16 [2048, 2880], P('ep', 'tp'), may hold values from -6 to 6
- expert_ids: int32 [2048, 4], P('ep'), may hold values from 0 to 15, all different within a row; in each aligned block of 256 rows (0 to 255, 256 to 511, ...) at most 128 rows name the same one
- combine_weights: float32 [2048, 4], P('ep'), may hold values from 0.05 to 0.6
- gate_weight: bfloat16 [16, 2880, 2880], P('ep', None, 'tp'), may hold values from -0.109375 to 0.109375
- up_weight: bfloat16 [16, 2880, 2880], P('ep', None, 'tp'), may hold values from -0.109375 to 0.109375
- down_weight: bfloat16 [16, 2880, 2880], P('ep', 'tp'), may hold values from -0.109375 to 0.109375
Outputs:
- mixed: bfloat16 [2048, 2880], P('ep', 'tp')
Inputs may be any that keep to these rules, and one draw needn't show every extreme that they name: `expert_ids`: each row names 4 different experts; within the 256 rows of one index of ep no expert is named more than 128 times, a bound that some block reaches.
All inputs are finite; a program needn't handle non-finite values.
Results may differ from a plain program's by a relative error of at most 0.014.
Values may be sent and summed in bfloat16 or wider, within the bound.
A program may use at most 128 MiB of HBM per device.

v0:
```python
import jax
import jax.numpy as jnp
from jax import lax
from jax.sharding import PartitionSpec as P


def activate(gate_acc, up_acc):
    return (up_acc + 1.0) * gate_acc * jax.nn.sigmoid(1.702 * gate_acc)


def local(tokens, expert_ids, combine_weights, gate_weight, up_weight, down_weight):
    ep_count = lax.axis_size("ep")
    exp_local = gate_weight.shape[0]
    experts = exp_local * ep_count
    tok_rows = expert_ids.shape[0]
    top_count = expert_ids.shape[1]
    capacity = 2 * tok_rows * top_count // experts
    feat_width = tokens.shape[1]
    flat_ids = expert_ids.reshape(-1)
    onehot = (flat_ids[:, None] == jnp.arange(experts, dtype=jnp.int32)[None, :]).astype(jnp.int32)
    slot_pos = jnp.sum((jnp.cumsum(onehot, axis=0) - onehot) * onehot, axis=1)
    expert_local = flat_ids % exp_local
    owner_dev = flat_ids // exp_local
    token_of = jnp.arange(tok_rows * top_count, dtype=jnp.int32) // top_count
    send_buf = jnp.zeros((exp_local, ep_count, capacity, feat_width), jnp.bfloat16)
    send_buf = send_buf.at[expert_local, owner_dev, slot_pos].set(tokens[token_of])
    arrived = lax.all_to_all(send_buf, "ep", split_axis=1, concat_axis=1, tiled=True)
    arrived = arrived.reshape(exp_local, ep_count * capacity, feat_width)
    shard_piece = lax.all_gather(arrived, "tp", axis=2, tiled=True)
    gate_new = jnp.einsum(
        "erd,edf->erf", shard_piece, gate_weight, preferred_element_type=jnp.float32
    )
    up_new = jnp.einsum("erd,edf->erf", shard_piece, up_weight, preferred_element_type=jnp.float32)
    hidden = activate(gate_new, up_new).astype(jnp.bfloat16)
    partials = jnp.einsum("erf,efd->erd", hidden, down_weight, preferred_element_type=jnp.float32)
    weights_flat = combine_weights.reshape(-1)
    summed = lax.psum_scatter(
        partials.astype(jnp.bfloat16), "tp", scatter_dimension=2, tiled=True
    ).astype(jnp.float32)
    summed = summed.reshape(exp_local, ep_count, capacity, summed.shape[2])
    returned = lax.all_to_all(
        summed.astype(jnp.bfloat16), "ep", split_axis=1, concat_axis=1, tiled=True
    ).astype(summed.dtype)
    picked = returned[expert_local, owner_dev, slot_pos]
    weighted = (picked * weights_flat[:, None]).reshape(tok_rows, top_count, picked.shape[1])
    mixed = jnp.sum(weighted, axis=1).astype(jnp.bfloat16)
    return mixed


def solution(mesh):
    in_specs = (
        P("ep", "tp"),
        P("ep", None),
        P("ep", None),
        P("ep", None, "tp"),
        P("ep", None, "tp"),
        P("ep", "tp", None),
    )
    out_specs = P("ep", "tp")
    return jax.shard_map(local, mesh=mesh, in_specs=in_specs, out_specs=out_specs, check_vma=False)
```

profile of v0, /device:TPU:0, one launch (start us, length us, event | category | flops | bytes accessed | tf_op | source)
XLA Modules:
  0.0 439.0 jit_solution(15752584724429517280)
XLA Ops:
  6.5 0.0 all-gather.2.cloned.1.call-start
  6.5 0.8 copy.44
  7.4 0.1 eq.31
  7.5 0.1 eq.27
  7.6 0.1 reshape.209
  7.8 4.5 %reduce-window.6 = s32[16,8,128]{2,1,0:T(8,128)S(1)} reduce-window(s32[16,8,128]{2,1,0:T(8,128)S(1)} %fusion.8, s32[]{:T(128)} %constant.48.clone.1), window={size=1x1x128 pad=0_0x0_0x127_0}, to_apply=%region_0.0 | reduce-window | flops 2080768 | bytes 131076 | tf_op jit(solution)/shard_map/reduce-window
  12.3 0.1 slice.13
  12.4 0.1 copy.47
  12.5 0.1 copy.48
  12.6 0.1 broadcast_add_fusion
  12.7 0.1 shift-left_or_fusion
  12.8 0.7 multiply_reduce_fusion.1
  13.5 0.7 and_reduce_fusion
  14.3 1.2 copy.49
  15.5 12.4 %scatter_custom_fusion = bf16[2048,720]{1,0:T(8,128)(2,1)S(1)} fusion(s32[1024]{0:T(1024)S(1)} %get-tuple-element.10, bf16[256,720]{1,0:T(8,128)(2,1)S(1)} %copy.49, s32[1024]{0:T(1024)S(1)} %get-tuple-element.9, bf16[]{:T(256)} %constant.47.clone.1), kind=kCustom, calls=%fused_computation.10 | custom fusion | bytes 2949122
  27.9 5.5 %copy.51 = bf16[2,8,128,720]{2,0,3,1:T(2,128)(2,1)} copy(bf16[2,8,128,720]{3,2,1,0:T(8,128)(2,1)S(1)} %bitcast.37) | data formatting | bytes 5898240 | tf_op jit(solution)/shard_map/scatter | solution.py:26
  33.5 74.4 %all_to_all.10 = bf16[2,8,128,720]{2,0,3,1:T(2,128)(2,1)S(1)} all-to-all(bf16[2,8,128,720]{2,0,3,1:T(2,128)(2,1)} %copy.51), channel_id=1, replica_groups=mesh['ep'=8,'tp'=4] {'ep'}, dimensions={1} | all-to-all | bytes 5898240 | tf_op jit(solution)/shard_map/all_to_all | solution.py:27
  107.8 1.1 copy.52
  109.0 3.3 reshape.211
  112.2 0.0 all-gather.2.cloned.1.call-update
  112.2 0.2 reduce-scatter.2.cloned.1.call-start
  112.5 76.0 %all-gather.2.cloned.1.call-done = bf16[2,1024,2880]{1,2,0:T(8,128)(2,1)} async-done(((bf16[2,1024,720]{1,2,0:T(8,128)(2,1)}), bf16[2,1024,2880]{1,2,0:T(8,128)(2,1)}) %all-gather.2.cloned.1.call-update) | async-done | bytes 11796496 | tf_op jit(solution)/shard_map/all_gather | solution.py:29
  188.5 16.2 %fusion.13 = f32[2,1024,720]{1,2,0:T(8,128)} fusion(bf16[2,2880,720]{1,2,0:T(8,128)(2,1)} %param.9, bf16[2,1024,2880]{1,2,0:T(8,128)(2,1)} %all-gather.2.cloned.1.call-done), kind=kOutput, calls=%fused_computation.43 | convolution fusion | flops 8493465600 | bytes 25989120 | tf_op jit(solution)/shard_map/erd,edf->erf/dot_general | solution.py:30
  204.6 27.0 %convolution_convert_fusion = bf16[2,1024,2880]{1,2,0:T(8,128)(2,1)} fusion(bf16[2,720,2880]{2,1,0:T(8,128)(2,1)} %param.11, f32[2,1024,720]{1,2,0:T(8,128)} %fusion.13, bf16[2,2880,720]{1,2,0:T(8,128)(2,1)} %param.10, bf16[2,1024,2880]{1,2,0:T(8,128)(2,1)} %all-gather.2.cloned.1.call-done), kind=kOutput, calls=%fused_computation.3 | convolution fusion | flops 17004625920 | bytes 46080000 | tf_op jit(solution)/shard_map/erf,efd->erd/dot_general | solution.py:35
  231.7 0.0 reduce-scatter.2.cloned.1.call-update
  231.7 0.0 copy-start
  231.7 93.6 %reduce-scatter.2.cloned.1.call-done = bf16[2,1024,720]{1,2,0:T(8,128)(2,1)} async-done(((bf16[2,1024,2880]{1,2,0:T(8,128)(2,1)}), bf16[2,1024,720]{1,2,0:T(8,128)(2,1)}) %reduce-scatter.2.cloned.1.call-update) | async-done | bytes 2949136 | tf_op jit(solution)/shard_map/reduce_scatter | solution.py:37
  325.3 4.0 copy_bitcast_fusion
  329.3 5.5 %all-to-all-start.1 = ((bf16[2,8,128,720]{2,3,0,1:T(8,128)(2,1)}), bf16[2,8,128,720]{2,3,0,1:T(8,128)(2,1)S(1)}, u32[]{:S(2)}, u32[]{:S(2)}) async-start(bf16[2,8,128,720]{2,3,0,1:T(8,128)(2,1)} %copy_bitcast_fusion), calls=%async_computation.2 | async-start | bytes 5898240 | tf_op jit(solution)/shard_map/all_to_all | solution.py:41
  334.8 0.0 copy-done
  334.8 0.1 copy.56
  335.0 66.2 %all-to-all-done.1 = bf16[2,8,128,720]{2,3,0,1:T(8,128)(2,1)S(1)} async-done(((bf16[2,8,128,720]{2,3,0,1:T(8,128)(2,1)}), bf16[2,8,128,720]{2,3,0,1:T(8,128)(2,1)S(1)}, u32[]{:S(2)}, u32[]{:S(2)}) %all-to-all-start.1) | async-done | bytes 2949152 | tf_op jit(solution)/shard_map/all_to_all | solution.py:41
  401.1 2.9 copy_convert_fusion
  404.1 6.5 %copy.55 = f32[2,8,128,720]{3,2,1,0:T(8,128)} copy(f32[2,8,128,720]{2,3,1,0:T(8,128)} %copy_convert_fusion) | data formatting | bytes 11796480 | tf_op jit(solution)/shard_map/convert_element_type | solution.py:43
  410.6 14.6 %gather_fusion = f32[1024,720]{1,0:T(8,128)S(1)} fusion(f32[2,8,128,720]{3,2,1,0:T(8,128)} %copy.55, s32[1024]{0:T(1024)S(1)} %bitcast.36), kind=kCustom, calls=%fused_computation.1 | custom fusion | bytes 5910528 | tf_op jit(solution)/shard_map/gather | solution.py:44
  425.2 2.1 gather.10
  427.3 3.9 multiply_reduce_fusion
  431.2 0.9 copy.57
  (6 shorter events, 0.1 us)
Async XLA Ops:
  6.5 181.9 %all-gather.2.cloned.1.call-start = ((), (), s32[]{:S(2)}) async-start(), calls=%async_computation.3 | async-start | bytes 14745600 | tf_op jit(solution)/shard_map/all_gather | solution.py:29
  112.2 213.1 %reduce-scatter.2.cloned.1.call-start = ((), (), s32[]{:S(2)}) async-start(), calls=%async_computation.4 | async-start | bytes 14745600 | tf_op jit(solution)/shard_map/reduce_scatter | solution.py:37
  231.7 103.1 %copy-start = (f32[256,4]{0,1:T(4,128)S(1)}, f32[256,4]{0,1:T(4,128)}, u32[]{:S(2)}) copy-start(f32[256,4]{0,1:T(4,128)} %param.8) | copy-start | bytes 12292
  329.3 71.8 %all-to-all-start.1 = ((bf16[2,8,128,720]{2,3,0,1:T(8,128)(2,1)}), bf16[2,8,128,720]{2,3,0,1:T(8,128)(2,1)S(1)}, u32[]{:S(2)}, u32[]{:S(2)}) async-start(bf16[2,8,128,720]{2,3,0,1:T(8,128)(2,1)} %copy_bitcast_fusion), calls=%async_computation.2 | async-start | bytes 5898240 | tf_op jit(solution)/shard_map/all_to_all | solution.py:41
Sparse Core Ops, SparseCore 0:
  112.4 76.0 all-gather.1
  231.8 93.4 reduce-scatter.1
where the time goes:
time: 440 us; the launch traced here: 439 us
  waiting for transfers between devices  236 us (54%)
  blocking collectives  74.4 us (17%)
  local copies, waits for them, and re-layouts  53.3 us (12%)
  matrix products  43.2 us (10%)
  between operations  13.5 us (3%)
  other arithmetic  13.1 us (3%)
  starting transfers between devices  5.73 us (1%)
    reduce_scatter x1, waiting for transfers between devices, local(): lax.psum_scatter(partials.astype(jnp.bfloat16), 'tp', scatter_dimension=2...  93.6 us
    all_gather x1, waiting for transfers between devices, local(): shard_piece = lax.all_gather(arrived, 'tp', axis=2, tiled=True)  76 us
    all_to_all x1, blocking collectives, local(): lax.all_to_all(send_buf, 'ep', split_axis=1, concat_axis=1, tiled=True)  74.4 us
    all_to_all x1, waiting for transfers between devices, local(): lax.all_to_all(summed.astype(jnp.bfloat16), 'ep', split_axis=1, concat_ax...  66.2 us
    dot_general x1, matrix products, local(): jnp.einsum('erf,efd->erd', hidden, down_weight, preferred_element_type=jn...  27 us
    gather x2, local copies, waits for them, and re-layouts, local(): picked = returned[expert_local, owner_dev, slot_pos]  16.7 us
    dot_general x1, matrix products, local(): jnp.einsum('erd,edf->erf', shard_piece, gate_weight, preferred_element_ty...  16.2 us
    unnamed x6, local copies, waits for them, and re-layouts  14.6 us
  transfers between devices with their start and end apart: 3, of which 3 were waited for; matrix products, arithmetic and copies ran while one was open for 0% of the time, Pallas kernels for 0%

commit v1 on v0

--- a/solution.py
+++ b/solution.py
@@ -2,6 +2,7 @@
 import jax.numpy as jnp
 from jax import lax
 from jax.sharding import PartitionSpec as P
+from jax.lax import all_to_all, axis_size
 
 
 def activate(gate_acc, up_acc):
@@ -24,7 +25,9 @@
     token_of = jnp.arange(tok_rows * top_count, dtype=jnp.int32) // top_count
     send_buf = jnp.zeros((exp_local, ep_count, capacity, feat_width), jnp.bfloat16)
     send_buf = send_buf.at[expert_local, owner_dev, slot_pos].set(tokens[token_of])
-    arrived = lax.all_to_all(send_buf, "ep", split_axis=1, concat_axis=1, tiled=True)
+    arrived = jnp.concatenate(
+        all_to_all(jnp.stack(jnp.split(send_buf, axis_size("ep"), axis=1)), "ep", 0, 0), axis=1
+    )
     arrived = arrived.reshape(exp_local, ep_count * capacity, feat_width)
     shard_piece = lax.all_gather(arrived, "tp", axis=2, tiled=True)
     gate_new = jnp.einsum(

time: 440 us -> 456 us (1.036)
  local copies, waits for them, and re-layouts: 53.3 us -> 68.9 us
    split x0 -> x9, local copies, waits for them, and re-layouts: none -> 15.8 us  [local(): jnp.split(send_buf, axis_size('ep'), axis=1)]
    scatter x1 -> x0, local copies, waits for them, and re-layouts: 5.54 us -> none  [local(): send_buf.at[expert_local, owner_dev, slot_pos].set(tokens[token_of])]
    unnamed x6 -> x19, local copies, waits for them, and re-layouts: 14.6 us -> 19.9 us
where the time goes in v1:
time: 456 us; the launch traced here: 455 us
  waiting for transfers between devices  236 us (52%)
  blocking collectives  74.2 us (16%)
  local copies, waits for them, and re-layouts  68.9 us (15%)
  matrix products  43.2 us (9%)
  between operations  13.6 us (3%)
  other arithmetic  13.1 us (3%)
  starting transfers between devices  5.86 us (1%)
    reduce_scatter x1, waiting for transfers between devices, local(): lax.psum_scatter(partials.astype(jnp.bfloat16), 'tp', scatter_dimension=2...  93.6 us
    all_gather x1, waiting for transfers between devices, local(): shard_piece = lax.all_gather(arrived, 'tp', axis=2, tiled=True)  76 us
    all_to_all x1, blocking collectives, local(): all_to_all(jnp.stack(jnp.split(send_buf, axis_size('ep'), axis=1)), 'ep',...  74.2 us
    all_to_all x1, waiting for transfers between devices, local(): lax.all_to_all(summed.astype(jnp.bfloat16), 'ep', split_axis=1, concat_ax...  66.2 us
    dot_general x1, matrix products, local(): jnp.einsum('erf,efd->erd', hidden, down_weight, preferred_element_type=jn...  27 us
    unnamed x19, local copies, waits for them, and re-layouts  19.9 us
    gather x2, local copies, waits for them, and re-layouts, local(): picked = returned[expert_local, owner_dev, slot_pos]  16.7 us
    dot_general x1, matrix products, local(): jnp.einsum('erd,edf->erf', shard_piece, gate_weight, preferred_element_ty...  16.2 us
  transfers between devices with their start and end apart: 3, of which 3 were waited for; matrix products, arithmetic and copies ran while one was open for 0% of the time, Pallas kernels for 0%

profile of v1, /device:TPU:0, one launch (start us, length us, event | category | flops | bytes accessed | tf_op | source)
XLA Modules:
  0.0 454.7 jit_solution(16088547828021151776)
XLA Ops:
  6.5 0.8 copy.203
  7.4 0.1 eq.31
  7.5 0.1 eq.27
  7.6 0.1 reshape.209
  7.8 4.5 reduce-window.6
  12.3 0.1 slice.13
  12.4 0.1 copy.206
  12.5 0.1 copy.207
  12.6 0.1 broadcast_add_fusion
  12.7 0.1 shift-left_or_fusion
  12.8 0.7 multiply_reduce_fusion.1
  13.5 0.7 and_reduce_fusion
  14.3 1.2 copy.208
  15.5 12.4 %scatter_custom_fusion = bf16[2048,720]{1,0:T(8,128)(2,1)S(1)} fusion(s32[1024]{0:T(1024)S(1)} %get-tuple-element.18, bf16[256,720]{1,0:T(8,128)(2,1)S(1)} %copy.208, s32[1024]{0:T(1024)S(1)} %get-tuple-element.17, bf16[]{:T(256)} %constant.47.clone.1), kind=kCustom, calls=%fused_computation.10 | custom fusion | bytes 2949122
  27.9 1.6 fusion.13
  29.5 1.9 copy.210
  31.4 1.0 bitcast_dynamic-update-slice_fusion.7
  32.4 1.9 copy.211
  34.3 1.9 copy.212
  36.2 1.9 copy.213
  38.1 1.9 copy.214
  40.0 1.9 copy.215
  42.0 1.9 copy.216
  43.9 0.9 copy.217
  44.8 1.1 bitcast_dynamic-update-slice_fusion.6
  45.9 1.0 bitcast_dynamic-update-slice_fusion.5
  46.9 1.0 bitcast_dynamic-update-slice_fusion.4
  48.0 1.0 bitcast_dynamic-update-slice_fusion.3
  49.0 0.1 bitcast_dynamic-update-slice_fusion.2
  49.2 0.1 bitcast_dynamic-update-slice_fusion
  49.2 74.2 %all_to_all.10 = bf16[8,2,1,128,720]{3,4,2,1,0:T(8,128)(2,1)S(1)} all-to-all(bf16[8,2,1,128,720]{3,4,2,1,0:T(8,128)(2,1)S(1)} %bitcast_dynamic-update-slice_fusion), channel_id=1, replica_groups=mesh['ep'=8,'tp'=4] {'ep'}, dimensions={0} | all-to-all | bytes 5898240 | tf_op jit(solution)/shard_map/all_to_all | solution.py:29
  123.4 1.1 copy.218
  124.5 3.3 reshape_reshape.3
  127.8 0.2 reduce-scatter.2.cloned.1.call-start
  128.0 76.0 %all-gather.2.cloned.1.call-done = bf16[2,1024,2880]{1,2,0:T(8,128)(2,1)} async-done(((bf16[2,1024,720]{1,2,0:T(8,128)(2,1)}), bf16[2,1024,2880]{1,2,0:T(8,128)(2,1)}) %all-gather.2.cloned.1.call-update) | async-done | bytes 11796496 | tf_op jit(solution)/shard_map/all_gather | solution.py:32
  204.0 16.2 %fusion.14 = f32[2,1024,720]{1,2,0:T(8,128)} fusion(bf16[2,2880,720]{1,2,0:T(8,128)(2,1)} %param.9, bf16[2,1024,2880]{1,2,0:T(8,128)(2,1)} %all-gather.2.cloned.1.call-done), kind=kOutput, calls=%fused_computation.52 | convolution fusion | flops 8493465600 | bytes 25989120 | tf_op jit(solution)/shard_map/erd,edf->erf/dot_general | solution.py:33
  220.2 27.0 %convolution_convert_fusion = bf16[2,1024,2880]{1,2,0:T(8,128)(2,1)} fusion(bf16[2,720,2880]{2,1,0:T(8,128)(2,1)} %param.11, f32[2,1024,720]{1,2,0:T(8,128)} %fusion.14, bf16[2,2880,720]{1,2,0:T(8,128)(2,1)} %param.10, bf16[2,1024,2880]{1,2,0:T(8,128)(2,1)} %all-gather.2.cloned.1.call-done), kind=kOutput, calls=%fused_computation.3 | convolution fusion | flops 17004625920 | bytes 46080000 | tf_op jit(solution)/shard_map/erf,efd->erd/dot_general | solution.py:38
  247.3 93.6 %reduce-scatter.2.cloned.1.call-done = bf16[2,1024,720]{1,2,0:T(8,128)(2,1)} async-done(((bf16[2,1024,2880]{1,2,0:T(8,128)(2,1)}), bf16[2,1024,720]{1,2,0:T(8,128)(2,1)}) %reduce-scatter.2.cloned.1.call-update) | async-done | bytes 2949136 | tf_op jit(solution)/shard_map/reduce_scatter | solution.py:40
  340.9 4.0 copy_bitcast_fusion
  344.9 5.6 %all-to-all-start.1 = ((bf16[2,8,128,720]{2,3,0,1:T(8,128)(2,1)}), bf16[2,8,128,720]{2,3,0,1:T(8,128)(2,1)S(1)}, u32[]{:S(2)}, u32[]{:S(2)}) async-start(bf16[2,8,128,720]{2,3,0,1:T(8,128)(2,1)} %copy_bitcast_fusion), calls=%async_computation.2 | async-start | bytes 5898240 | tf_op jit(solution)/shard_map/all_to_all | solution.py:44
  350.5 0.1 copy.222
  350.6 66.2 %all-to-all-done.1 = bf16[2,8,128,720]{2,3,0,1:T(8,128)(2,1)S(1)} async-done(((bf16[2,8,128,720]{2,3,0,1:T(8,128)(2,1)}), bf16[2,8,128,720]{2,3,0,1:T(8,128)(2,1)S(1)}, u32[]{:S(2)}, u32[]{:S(2)}) %all-to-all-start.1) | async-done | bytes 2949152 | tf_op jit(solution)/shard_map/all_to_all | solution.py:44
  416.8 2.9 copy_convert_fusion
  419.8 6.5 %copy.221 = f32[2,8,128,720]{3,2,1,0:T(8,128)} copy(f32[2,8,128,720]{2,3,1,0:T(8,128)} %copy_convert_fusion) | data formatting | bytes 11796480 | tf_op jit(solution)/shard_map/convert_element_type | solution.py:46
  426.2 14.6 %gather_fusion = f32[1024,720]{1,0:T(8,128)S(1)} fusion(f32[2,8,128,720]{3,2,1,0:T(8,128)} %copy.221, s32[1024]{0:T(1024)S(1)} %bitcast.53), kind=kCustom, calls=%fused_computation.1 | custom fusion | bytes 5910528 | tf_op jit(solution)/shard_map/gather | solution.py:47
  440.8 2.2 gather.10
  443.0 3.9 multiply_reduce_fusion
  446.9 0.9 copy.223
  (18 shorter events, 0.2 us)
Async XLA Ops:
  6.5 197.5 %all-gather.2.cloned.1.call-start = ((), (), s32[]{:S(2)}) async-start(), calls=%async_computation.3 | async-start | bytes 14745600 | tf_op jit(solution)/shard_map/all_gather | solution.py:32
  44.8 4.3 copy-start.2
  44.8 4.3 copy-start
  44.8 4.4 copy-start.1
  127.8 213.1 %reduce-scatter.2.cloned.1.call-start = ((), (), s32[]{:S(2)}) async-start(), calls=%async_computation.4 | async-start | bytes 14745600 | tf_op jit(solution)/shard_map/reduce_scatter | solution.py:40
  344.9 5.6 %copy-start.3 = (f32[256,4]{0,1:T(4,128)S(1)}, f32[256,4]{0,1:T(4,128)}, u32[]{:S(2)}) copy-start(f32[256,4]{0,1:T(4,128)} %param.8) | copy-start | bytes 12292
  344.9 72.0 %all-to-all-start.1 = ((bf16[2,8,128,720]{2,3,0,1:T(8,128)(2,1)}), bf16[2,8,128,720]{2,3,0,1:T(8,128)(2,1)S(1)}, u32[]{:S(2)}, u32[]{:S(2)}) async-start(bf16[2,8,128,720]{2,3,0,1:T(8,128)(2,1)} %copy_bitcast_fusion), calls=%async_computation.2 | async-start | bytes 5898240 | tf_op jit(solution)/shard_map/all_to_all | solution.py:44
Sparse Core Ops, SparseCore 0:
  127.9 76.0 all-gather.1
  247.4 93.4 reduce-scatter.1
